TPU v7x, 32 devices: a whole 2x2x4 slice. The times are simulated.
32 devices in a mesh: gx: 4 (over x, core), gy: 2 (over y), gz: 4 (over z).
Axes of the slice: x: 2, y: 2, z: 4, core: 2. Of those that a mesh axis runs over, the one named last changes fastest.
Arguments:
- velocity: float32 [3, 128, 192, 1024], P(None, 'gx', 'gy', 'gz'), may hold values from -6 to 6
Outputs:
- magnitude: float32 [128, 192, 1024], P('gx', ('gy', 'gz'))
- level_one: float32 [64, 96, 512], P('gx', 'gy')
- level_two: float32 [32, 48, 256], P('gx', 'gy')
- level_three: float32 [16, 24, 128], P('gx', 'gy')
- level_four: float32 [8, 12, 64], P('gx', 'gy')
- level_five: float32 [4, 6, 32], P('gx', 'gy')
All inputs are finite; a program needn't handle non-finite values.
Results may differ from a plain program's by a relative error of at most 0.000075.
Values sent between devices are 32-bit elements; how exact they have to be, the bound alone decides.
A program may use at most 256 MiB of HBM per device.

v0:
```python
import jax
import jax.numpy as jnp
from jax import lax
from jax.sharding import PartitionSpec as P


def extended(value, sides, width):
    for axis, dim in sides:
        peers, length = (lax.axis_size(axis), value.shape[dim])
        up = [(i, (i + 1) % peers) for i in range(peers)]
        down = [(j, i) for i, j in up]
        last = lax.slice_in_dim(value, length - width, length, axis=dim)
        leading = lax.slice_in_dim(value, 0, width, axis=dim)
        before = lax.ppermute(last, axis, up)
        after = lax.ppermute(leading, axis, down)
        value = jnp.concatenate([before, value, after], axis=dim)
    return value


def depth_diff(field, before, after):
    ahead = jnp.roll(field, -1, 2)
    behind = jnp.roll(field, 1, 2)
    depth_index = lax.broadcasted_iota(jnp.int32, field.shape, 2)
    ahead = jnp.where(depth_index == field.shape[2] - 1, after[:, :, None], ahead)
    behind = jnp.where(depth_index == 0, before[:, :, None], behind)
    return (ahead - behind) * 0.5


def vorticity(padded, before, after):
    inner = padded[:, 1:-1, 1:-1, :]

    def first_diff(comp):
        return (padded[comp, 2:, 1:-1, :] - padded[comp, :-2, 1:-1, :]) * 0.5

    def second_diff(comp):
        return (padded[comp, 1:-1, 2:, :] - padded[comp, 1:-1, :-2, :]) * 0.5

    def third_diff(comp):
        return depth_diff(inner[comp], before[comp], after[comp])

    curl_first = second_diff(2) - third_diff(1)
    curl_second = third_diff(0) - first_diff(2)
    curl_third = first_diff(1) - second_diff(0)
    return jnp.sqrt(
        1.0 + curl_first * curl_first + curl_second * curl_second + curl_third * curl_third
    )


def pooled(field):
    rows, cols, depth = field.shape
    summed = field.reshape(rows // 2, 2, cols, depth).sum(axis=1)
    summed = summed.reshape(rows // 2, cols // 2, 2, depth).sum(axis=2)
    pairing = (
        lax.broadcasted_iota(jnp.int32, (depth, depth // 2), 0) // 2
        == lax.broadcasted_iota(jnp.int32, (depth, depth // 2), 1)
    ).astype(jnp.float32)
    merged = jnp.dot(
        summed.reshape(-1, depth),
        pairing,
        precision=lax.Precision.HIGHEST,
        preferred_element_type=jnp.float32,
    )
    return merged.reshape(rows // 2, cols // 2, depth // 2) * 0.125


def end_planes(velocity):
    return jnp.concatenate([velocity[..., :1], velocity[..., -1:]], axis=3)


def on_device(velocity):
    padded = extended(velocity, (("gx", 1), ("gy", 2)), 1)
    planes = extended(end_planes(velocity), (("gz", 3),), 1)
    block_mag = vorticity(padded, planes[..., 0], planes[..., 3])
    pencil = lax.all_to_all(block_mag, "gz", split_axis=1, concat_axis=2, tiled=True)
    level_one = lax.all_gather(pooled(pencil), "gz", axis=1, tiled=True)
    level_two = pooled(level_one)
    level_three = pooled(level_two)
    level_four = pooled(level_three)
    level_five = pooled(level_four)
    return (pencil, level_one, level_two, level_three, level_four, level_five)


def solution(mesh):
    in_specs = (P(None, "gx", "gy", "gz"),)
    out_specs = (
        P("gx", ("gy", "gz"), None),
        P("gx", "gy", None),
        P("gx", "gy", None),
        P("gx", "gy", None),
        P("gx", "gy", None),
        P("gx", "gy", None),
    )
    return jax.shard_map(
        on_device, mesh=mesh, in_specs=in_specs, out_specs=out_specs, check_vma=False
    )
```

profile of v0, /device:TPU:0, one launch (start us, length us, event | category | flops | bytes accessed | tf_op | source)
XLA Modules:
  0.0 252.0 jit_solution(13280708438288536689)
XLA Ops:
  9.3 2.4 collective-permute-start.1
  12.8 8.7 %fusion.60 = (f32[3,32,96,1]{3,2,1,0:T(8,128)}, f32[3,32,96,1]{3,2,1,0:T(8,128)}) fusion(f32[3,32,96,256]{3,2,1,0:T(8,128)} %param.1), kind=kLoop, calls=%fused_computation.114 | loop fusion | bytes 147456 | tf_op jit(solution)/shard_map/slice | solution.py:67
  21.5 3.1 %copy.129 = f32[3,32,96,1]{2,1,3,0:T(8,128)S(1)} copy(f32[3,32,96,1]{3,2,1,0:T(8,128)} %get-tuple-element.51) | data formatting | bytes 73728
  24.6 1.6 collective-permute-start.5
  26.2 3.1 %copy.128 = f32[3,32,96,1]{2,1,3,0:T(8,128)S(1)} copy(f32[3,32,96,1]{3,2,1,0:T(8,128)} %get-tuple-element.50) | data formatting | bytes 73728
  29.3 2.5 collective-permute-start.4
  31.8 16.0 %constant_dynamic-update-slice_fusion = (f32[3,33,96,256]{3,1,2,0:T(8,128)}, f32[3,32,96,256]{3,1,2,0:T(8,128)}) fusion(f32[3,32,96,256]{3,2,1,0:T(8,128)} %param.1), kind=kLoop, calls=%fused_computation.93 | loop fusion | bytes 28311552
  47.7 3.6 %slice_bitcast_fusion = (f32[32,96,256]{2,0,1:T(8,128)S(1)}, f32[32,96,256]{2,0,1:T(8,128)S(1)}) fusion(f32[3,32,96,256]{3,1,2,0:T(8,128)} %get-tuple-element.55), kind=kLoop, calls=%fused_computation.22 | loop fusion | bytes 12582912 | tf_op jit(solution)/shard_map/squeeze | solution.py:39
  51.3 3.7 %fusion.62 = (f32[32,96,1]{2,0,1:T(8,128)}, f32[32,96,1]{2,0,1:T(8,128)}, f32[32,96,1]{2,0,1:T(8,128)}, f32[32,96,1]{2,0,1:T(8,128)}) fusion(f32[32,96,256]{2,0,1:T(8,128)S(1)} %get-tuple-element.52, f32[32,96,256]{2,0,1:T(8,128)S(1)} %get-tuple-element.53), kind=kLoop, calls=%fused_computation.116 | loop fusion | bytes 98304 | tf_op jit(solution)/shard_map/jit(_roll_static)/slice | solution.py:22
  55.0 6.5 %fusion.63 = (f32[32,96,255]{2,0,1:T(8,128)}, f32[32,96,255]{2,0,1:T(8,128)}, f32[32,96,255]{2,0,1:T(8,128)}, f32[32,96,255]{2,0,1:T(8,128)}) fusion(f32[32,96,256]{2,0,1:T(8,128)S(1)} %get-tuple-element.52, f32[32,96,256]{2,0,1:T(8,128)S(1)} %get-tuple-element.53), kind=kLoop, calls=%fused_computation.117 | loop fusion | bytes 25067520 | tf_op jit(solution)/shard_map/jit(_roll_static)/slice | solution.py:22
  62.8 1.8 pad_maximum_fusion.9
  64.7 1.5 collective-permute-start.2
  66.7 1.3 slice_bitcast_fusion.5
  68.2 1.4 copy.106
  69.6 1.4 copy.110
  71.1 7.8 %dynamic-update-slice.1 = f32[3,33,96,256]{3,1,2,0:T(8,128)} dynamic-update-slice(f32[3,33,96,256]{3,1,2,0:T(8,128)} %get-tuple-element.54, f32[3,1,96,256]{3,1,2,0:T(1,128)S(1)} %collective-permute-done.1, s32[]{} %constant.86, s32[]{} %constant.87, s32[]{} %constant.86, s32[]{} %constant.86) | dynamic-update-slice | bytes 589828 | tf_op jit(solution)/shard_map/concatenate | solution.py:16
  78.9 21.6 %fusion.6 = f32[32,96,256]{2,0,1:T(8,128)} fusion(f32[3,34,1,256]{3,1,2,0:T(8,128)} %collective-permute-done.3, f32[3,1,96,256]{3,1,2,0:T(1,128)S(1)} %collective-permute-done.1, f32[3,32,96,256]{3,1,2,0:T(8,128)} %get-tuple-element.55, f32[3,1,96,256]{3,1,2,0:T(1,128)} %collective-permute-done, f32[3,34,1,256]{3,1,2,0:T(8,128)} %collective-permute-done.2, ...), kind=kLoop, calls=%fused_computation.7 | loop fusion | flops 33816576 | bytes 32305664 | tf_op jit(solution)/shard_map/sqrt | solution.py:44
  100.5 3.7 %all-to-all-start = ((f32[32,96,256]{2,0,1:T(8,128)}), f32[32,96,256]{2,0,1:T(8,128)S(1)}, u32[]{:S(2)}, u32[]{:S(2)}) async-start(f32[32,96,256]{2,0,1:T(8,128)} %fusion.6), calls=%async_computation | async-start | bytes 6291456 | tf_op jit(solution)/shard_map/all_to_all | solution.py:74
  104.3 70.6 %all-to-all-done = f32[32,96,256]{2,0,1:T(8,128)S(1)} async-done(((f32[32,96,256]{2,0,1:T(8,128)}), f32[32,96,256]{2,0,1:T(8,128)S(1)}, u32[]{:S(2)}, u32[]{:S(2)}) %all-to-all-start) | async-done | bytes 3145760 | tf_op jit(solution)/shard_map/all_to_all | solution.py:74
  175.0 1.7 copy-done.1
  176.6 3.9 %copy.145 = f32[32,4,24,256]{3,1,2,0:T(4,128)S(1)} copy(f32[32,4,24,256]{3,0,2,1:T(8,128)} %bitcast.78) | data formatting | bytes 6291456 | tf_op jit(solution)/shard_map/all_to_all | solution.py:74
  180.5 3.3 %reshape.90 = f32[16,2,24,1024]{3,2,1,0:T(8,128)} reshape(f32[32,24,4,256]{3,2,1,0:T(4,128)S(1)} %bitcast.76) | data formatting | bytes 6291456 | tf_op jit(solution)/shard_map/reshape | solution.py:51
  183.8 3.5 %reduce_sum.90 = f32[16,24,1024]{2,1,0:T(8,128)} reduce(f32[16,2,24,1024]{3,2,1,0:T(8,128)} %reshape.90, f32[]{:T(128)} %constant.81.clone.1), dimensions={1}, to_apply=%region_0.1 | reduce | flops 393216 | bytes 4718596 | tf_op jit(solution)/shard_map/reduce_sum | solution.py:51
  187.3 3.5 %copy.126 = f32[16,24,1024]{2,0,1:T(8,128)} copy(f32[16,24,1024]{2,1,0:T(8,128)} %reduce_sum.90) | data formatting | bytes 3145728 | tf_op jit(solution)/shard_map/reshape | solution.py:52
  190.8 2.5 reduce_sum.91
  193.2 3.0 %fusion.26 = f32[16,12,512]{2,0,1:T(8,128)} fusion(f32[16,12,1024]{2,0,1:T(8,128)} %reduce_sum.91, s32[1024]{0:T(1024)S(1)} %get-tuple-element.82, s32[1024]{0:T(1024)S(1)} %get-tuple-element.83, pred[1024]{0:T(1024)(128)(4,1)S(1)} %fusion.56), kind=kOutput, calls=%fused_computation.42 | convolution fusion | flops 1209106432 | bytes 1188864 | tf_op jit(solution)/shard_map/dot_general | solution.py:57
  196.4 3.0 %all_to_all.16 = f32[32,24,1024]{2,1,0:T(8,128)} reshape(f32[32,24,4,256]{3,2,1,0:T(4,128)S(1)} %bitcast.77) | data formatting | bytes 6291456 | tf_op jit(solution)/shard_map/all_to_all | solution.py:74
  199.4 33.1 %all-gather.2.cloned.1.call-done = f32[16,48,512]{2,0,1:T(8,128)} async-done(((f32[16,12,512]{2,0,1:T(8,128)}), f32[16,48,512]{2,0,1:T(8,128)}) %all-gather.2.cloned.1.call-update) | async-done | bytes 1572880 | tf_op jit(solution)/shard_map/all_gather | solution.py:75
  232.6 2.2 reshape.92
  234.8 3.0 %reduce_sum.92 = f32[8,48,512]{2,0,1:T(8,128)} reduce(f32[8,2,48,512]{3,1,0,2:T(2,128)S(1)} %reshape.92, f32[]{:T(128)} %constant.81.clone.1), dimensions={1}, to_apply=%region_2.3 | reduce | flops 196608 | bytes 2359300 | tf_op jit(solution)/shard_map/reduce_sum | solution.py:51
  239.0 1.4 bitcast_reduce_fusion
  243.1 2.1 copy.122
  (45 shorter events, 9.1 us)
Async XLA Ops:
  9.3 53.5 %collective-permute-start.1 = (f32[3,1,96,256]{3,1,2,0:T(1,128)}, f32[3,1,96,256]{3,1,2,0:T(1,128)S(1)}, u32[]{:S(2)}, u32[]{:S(2)}) collective-permute-start(f32[3,1,96,256]{3,1,2,0:T(1,128)} %copy.103), channel_id=1, source_target_pairs={{8,0},{16,8},{24,16},{0,24},{9,1},{17,9},{25,17},{1,25},{10,2},{18... | collective-permute-start | bytes 884744 | tf_op jit(solution)/shard_map/ppermute | solution.py:15
  12.8 50.1 %collective-permute-start = (f32[3,1,96,256]{3,1,2,0:T(1,128)}, f32[3,1,96,256]{3,1,2,0:T(1,128)}, u32[]{:S(2)}, u32[]{:S(2)}) collective-permute-start(f32[3,1,96,256]{3,1,2,0:T(1,128)} %copy.102), channel_id=1, source_target_pairs={{0,8},{8,16},{16,24},{24,0},{1,9},{9,17},{17,25},{25,1},{2,10},{10... | collective-permute-start | bytes 884744 | tf_op jit(solution)/shard_map/ppermute | solution.py:14
  24.6 37.5 %collective-permute-start.5 = (f32[3,32,96,1]{2,1,3,0:T(8,128)S(1)}, f32[3,32,96,1]{2,1,3,0:T(8,128)}, u32[]{:S(2)}, u32[]{:S(2)}) collective-permute-start(f32[3,32,96,1]{2,1,3,0:T(8,128)S(1)} %copy.129), channel_id=1, source_target_pairs={{0,1},{1,2},{2,3},{3,0},{4,5},{5,6},{6,7},{7,4},{8,9},{9,10},{10,1... | collective-permute-start | bytes 110600 | tf_op jit(solution)/shard_map/ppermute | solution.py:14
  29.3 37.4 %collective-permute-start.4 = (f32[3,32,96,1]{2,1,3,0:T(8,128)S(1)}, f32[3,32,96,1]{2,1,3,0:T(8,128)}, u32[]{:S(2)}, u32[]{:S(2)}) collective-permute-start(f32[3,32,96,1]{2,1,3,0:T(8,128)S(1)} %copy.128), channel_id=1, source_target_pairs={{1,0},{2,1},{3,2},{0,3},{5,4},{6,5},{7,6},{4,7},{9,8},{10,9},{11,1... | collective-permute-start | bytes 110600 | tf_op jit(solution)/shard_map/ppermute | solution.py:15
  62.8 16.1 %copy-start = (f32[32,96,255]{2,0,1:T(8,128)S(1)}, f32[32,96,255]{2,0,1:T(8,128)}, u32[]{:S(2)}) copy-start(f32[32,96,255]{2,0,1:T(8,128)} %get-tuple-element.60) | copy-start | bytes 9400324
  64.7 14.2 %collective-permute-start.2 = (f32[3,34,1,256]{3,1,2,0:T(8,128)}, f32[3,34,1,256]{3,1,2,0:T(8,128)}, u32[]{:S(2)}, u32[]{:S(2)}) collective-permute-start(f32[3,34,1,256]{3,1,2,0:T(8,128)} %get-tuple-element.48), channel_id=1, source_target_pairs={{4,0},{0,4},{5,1},{1,5},{6,2},{2,6},{7,3},{3,7},{12,8},{8,12},{13,... | collective-permute-start | bytes 313352 | tf_op jit(solution)/shard_map/ppermute | solution.py:15
  66.2 12.7 %collective-permute-start.3 = (f32[3,34,1,256]{3,1,2,0:T(8,128)}, f32[3,34,1,256]{3,1,2,0:T(8,128)}, u32[]{:S(2)}, u32[]{:S(2)}) collective-permute-start(f32[3,34,1,256]{3,1,2,0:T(8,128)} %get-tuple-element.49), channel_id=1, source_target_pairs={{0,4},{4,0},{1,5},{5,1},{2,6},{6,2},{3,7},{7,3},{8,12},{12,8},{9,1... | collective-permute-start | bytes 313352 | tf_op jit(solution)/shard_map/ppermute | solution.py:14
  100.5 74.4 %all-to-all-start = ((f32[32,96,256]{2,0,1:T(8,128)}), f32[32,96,256]{2,0,1:T(8,128)S(1)}, u32[]{:S(2)}, u32[]{:S(2)}) async-start(f32[32,96,256]{2,0,1:T(8,128)} %fusion.6), calls=%async_computation | async-start | bytes 6291456 | tf_op jit(solution)/shard_map/all_to_all | solution.py:74
  104.2 128.3 %all-gather.2.cloned.1.call-start = ((), (), s32[]{:S(2)}) async-start(), calls=%async_computation.1 | async-start | bytes 1966080 | tf_op jit(solution)/shard_map/all_gather | solution.py:75
  175.0 1.7 copy-start.1
  234.8 8.3 %copy-start.2 = (f32[16,48,512]{2,0,1:T(8,128)S(1)}, f32[16,48,512]{2,0,1:T(8,128)}, u32[]{:S(2)}) copy-start(f32[16,48,512]{2,0,1:T(8,128)} %all-gather.2.cloned.1.call-done) | copy-start | bytes 4718596
Sparse Core Ops, SparseCore 0:
  196.4 36.0 all-gather.1
where the time goes:
time: 253 us; the launch traced here: 252 us
  waiting for transfers between devices  104 us (41%)
  local copies, waits for them, and re-layouts  82.3 us (33%)
  other arithmetic  34.2 us (14%)
  between operations  14.2 us (6%)
  starting transfers between devices  12.3 us (5%)
  matrix products  5.12 us (2%)
    all_to_all x1, waiting for transfers between devices, on_device(): lax.all_to_all(block_mag, 'gz', split_axis=1, concat_axis=2, tiled=True)  70.6 us
    all_gather x1, waiting for transfers between devices, on_device(): level_one = lax.all_gather(pooled(pencil), 'gz', axis=1, tiled=True)  33.1 us
    unnamed x13, local copies, waits for them, and re-layouts  27.7 us
    sqrt x1, other arithmetic, vorticity(): jnp.sqrt(1.0 + curl_first * curl_first + curl_second * curl_second + curl...  21.6 us
    slice x2, local copies, waits for them, and re-layouts, depth_diff(): behind = jnp.roll(field, 1, 2)  10.2 us
    slice x1, local copies, waits for them, and re-layouts, end_planes(): return jnp.concatenate([velocity[..., :1], velocity[..., -1:]], axis=3)  8.69 us
    concatenate x1, local copies, waits for them, and re-layouts, extended(): value = jnp.concatenate([before, value, after], axis=dim)  7.82 us
    all_to_all x2, local copies, waits for them, and re-layouts, on_device(): lax.all_to_all(block_mag, 'gz', split_axis=1, concat_axis=2, tiled=True)  6.95 us
  transfers between devices with their start and end apart: 8, of which 2 were waited for; matrix products, arithmetic and copies ran while one was open for 24% of the time, Pallas kernels for 0%

commit v1 on v0

--- a/solution.py
+++ b/solution.py
@@ -71,7 +71,10 @@
     padded = extended(velocity, (("gx", 1), ("gy", 2)), 1)
     planes = extended(end_planes(velocity), (("gz", 3),), 1)
     block_mag = vorticity(padded, planes[..., 0], planes[..., 3])
-    pencil = lax.all_to_all(block_mag, "gz", split_axis=1, concat_axis=2, tiled=True)
+    pencil = jnp.concatenate(
+        lax.all_to_all(jnp.stack(jnp.split(block_mag, lax.axis_size("gz"), axis=1)), "gz", 0, 0),
+        axis=2,
+    )
     level_one = lax.all_gather(pooled(pencil), "gz", axis=1, tiled=True)
     level_two = pooled(level_one)
     level_three = pooled(level_two)

time: 253 us -> 245 us (0.968)
  local copies, waits for them, and re-layouts: 82.3 us -> 75.3 us
  other arithmetic: 34.2 us -> 29 us
  waiting for transfers between devices: 104 us -> 107 us
    slice x2, local copies, waits for them, and re-layouts: 10.2 us -> 17.2 us  [depth_diff(): behind = jnp.roll(field, 1, 2)]
    concatenate x1, local copies, waits for them, and re-layouts: 7.82 us -> 0.87 us  [extended(): value = jnp.concatenate([before, value, after], axis=dim)]
    all_to_all x2 -> x0, local copies, waits for them, and re-layouts: 6.95 us -> none  [on_device(): lax.all_to_all(block_mag, 'gz', split_axis=1, concat_axis=2, tiled=True)]
    reshape x0 -> x2, local copies, waits for them, and re-layouts: none -> 5.83 us  [on_device(): jnp.concatenate(lax.all_to_all(jnp.stack(jnp.split(block_mag, lax.axis_si...]
    another operation x0 -> x2, local copies, waits for them, and re-layouts: none -> 5.47 us  [the longest x1 5.23 us: pooled(): summed = field.reshape(rows // 2, 2, cols, depth).sum(axis=1)]
    unnamed x13 -> x20, local copies, waits for them, and re-layouts: 27.7 us -> 22.5 us
    sqrt x1, other arithmetic: 21.6 us -> 16.8 us  [vorticity(): jnp.sqrt(1.0 + curl_first * curl_first + curl_second * curl_second + curl...]
    broadcast_in_dim x3 -> x1, local copies, waits for them, and re-layouts: 4.2 us -> 0.01 us  [depth_diff(): jnp.where(depth_index == field.shape[2] - 1, after[:, :, None], ahead)]
  transfers between devices with their start and end apart: 8 -> 8, of which waited for: 2 -> 4; matrix products, arithmetic and copies ran while one was open for 24% -> 23% of each run, Pallas kernels for 0% -> 0%
where the time goes in v1:
time: 245 us; the launch traced here: 244 us
  waiting for transfers between devices  107 us (44%)
  local copies, waits for them, and re-layouts  75.3 us (31%)
  other arithmetic  29 us (12%)
  between operations  14.2 us (6%)
  starting transfers between devices  13.9 us (6%)
  matrix products  5.1 us (2%)
    all_to_all x1, waiting for transfers between devices, on_device(): lax.all_to_all(jnp.stack(jnp.split(block_mag, lax.axis_size('gz'), axis=1...  69.4 us
    all_gather x1, waiting for transfers between devices, on_device(): level_one = lax.all_gather(pooled(pencil), 'gz', axis=1, tiled=True)  32.9 us
    unnamed x20, local copies, waits for them, and re-layouts  22.5 us
    slice x2, local copies, waits for them, and re-layouts, depth_diff(): behind = jnp.roll(field, 1, 2)  17.2 us
    sqrt x1, other arithmetic, vorticity(): jnp.sqrt(1.0 + curl_first * curl_first + curl_second * curl_second + curl...  16.8 us
    slice x1, local copies, waits for them, and re-layouts, end_planes(): return jnp.concatenate([velocity[..., :1], velocity[..., -1:]], axis=3)  8.74 us
    ppermute x3, starting transfers between devices, extended(): after = lax.ppermute(leading, axis, down)  7.96 us
    reduce_sum x2, other arithmetic, pooled(): summed = field.reshape(rows // 2, 2, cols, depth).sum(axis=1)  6.46 us
  transfers between devices with their start and end apart: 8, of which 4 were waited for; matrix products, arithmetic and copies ran while one was open for 23% of the time, Pallas kernels for 0%

profile of v1, /device:TPU:0, one launch (start us, length us, event | category | flops | bytes accessed | tf_op | source)
XLA Modules:
  0.0 244.4 jit_solution(10105554741993692881)
XLA Ops:
  7.2 1.1 fusion.61
  8.8 2.0 collective-permute-start.1
  10.8 8.7 %fusion.60 = (f32[3,32,96,1]{3,2,1,0:T(8,128)}, f32[3,32,96,1]{3,2,1,0:T(8,128)}) fusion(f32[3,32,96,256]{3,2,1,0:T(8,128)} %param.1), kind=kLoop, calls=%fused_computation.117 | loop fusion | bytes 147456 | tf_op jit(solution)/shard_map/slice | solution.py:67
  19.5 3.1 %copy.69 = f32[3,32,96,1]{2,1,3,0:T(8,128)S(1)} copy(f32[3,32,96,1]{3,2,1,0:T(8,128)} %get-tuple-element.44) | data formatting | bytes 73728
  22.6 4.4 %collective-permute-start.4 = (f32[3,32,96,1]{2,1,3,0:T(8,128)S(1)}, f32[3,32,96,1]{2,1,3,0:T(8,128)S(1)}, u32[]{:S(2)}, u32[]{:S(2)}) collective-permute-start(f32[3,32,96,1]{2,1,3,0:T(8,128)S(1)} %copy.69), channel_id=1, source_target_pairs={{1,0},{2,1},{3,2},{0,3},{5,4},{6,5},{7,6},{4,7},{9,8},{10,9},{11,1... | collective-permute-start | bytes 110600 | tf_op jit(solution)/shard_map/ppermute | solution.py:15
  27.0 3.1 %copy.70 = f32[3,32,96,1]{2,1,3,0:T(8,128)S(1)} copy(f32[3,32,96,1]{3,2,1,0:T(8,128)} %get-tuple-element.45) | data formatting | bytes 73728
  30.2 6.3 %slice_bitcast_fusion = (f32[32,96,256]{2,1,0:T(8,128)}, f32[32,96,256]{2,1,0:T(8,128)}) fusion(f32[3,32,96,256]{3,2,1,0:T(8,128)} %param.1), kind=kLoop, calls=%fused_computation.32 | loop fusion | bytes 12582912 | tf_op jit(solution)/shard_map/squeeze | solution.py:39
  36.5 11.1 %fusion.63 = (f32[32,96,255]{2,1,0:T(8,128)}, f32[32,96,255]{2,1,0:T(8,128)}, f32[32,96,255]{2,1,0:T(8,128)}, f32[32,96,255]{2,1,0:T(8,128)}) fusion(f32[32,96,256]{2,1,0:T(8,128)} %get-tuple-element.46, f32[32,96,256]{2,1,0:T(8,128)} %get-tuple-element.47), kind=kLoop, calls=%fused_computation.120 | loop fusion | bytes 25067520 | tf_op jit(solution)/shard_map/jit(_roll_static)/slice | solution.py:22
  47.6 6.1 %fusion.62 = (f32[32,96,1]{2,1,0:T(8,128)S(1)}, f32[32,96,1]{2,1,0:T(8,128)}, f32[32,96,1]{2,1,0:T(8,128)}, f32[32,96,1]{2,1,0:T(8,128)}) fusion(f32[32,96,256]{2,1,0:T(8,128)} %get-tuple-element.46, f32[32,96,256]{2,1,0:T(8,128)} %get-tuple-element.47), kind=kLoop, calls=%fused_computation.119 | loop fusion | bytes 98304 | tf_op jit(solution)/shard_map/jit(_roll_static)/slice | solution.py:22
  53.7 0.9 constant_dynamic-update-slice_fusion.6
  54.6 11.5 %constant_dynamic-update-slice_fusion.4 = (f32[3,33,96,256]{3,2,1,0:T(8,128)}, f32[3,34,96,256]{3,2,1,0:T(8,128)}, f32[3,33,96,256]{3,2,1,0:T(8,128)}) fusion(f32[3,32,96,256]{3,2,1,0:T(8,128)S(1)} %bitcast.84, f32[3,34,96,256]{3,2,1,0:T(8,128)} %get-tuple-element.68, f32[3,33,96,256]{3,2,1,0:T(8,128)} %get-tuple-element.67), kind=kLoop, calls=%fused_computation.75 | loop fusion | bytes 37748736
  67.0 1.6 fusion.59
  68.6 1.6 collective-permute-start.2
  70.7 3.6 %collective-permute-done.2 = f32[3,34,1,256]{3,2,1,0:T(1,128)S(1)} collective-permute-done((f32[3,34,1,256]{3,2,1,0:T(1,128)S(1)}, f32[3,34,1,256]{3,2,1,0:T(1,128)S(1)}, u32[]{:S(2)}, u32[]{:S(2)}) %collective-permute-start.2) | collective-permute-done | bytes 104480 | tf_op jit(solution)/shard_map/ppermute | solution.py:15
  74.3 1.1 collective-permute-done.3
  75.4 16.8 %fusion.6 = f32[32,96,256]{2,1,0:T(8,128)S(1)} fusion(f32[3,34,96,256]{3,2,1,0:T(8,128)} %get-tuple-element.66, f32[3,34,1,256]{3,2,1,0:T(1,128)S(1)} %collective-permute-done.3, f32[3,34,1,256]{3,2,1,0:T(1,128)S(1)} %collective-permute-done.2, f32[3,33,96,256]{3,2,1,0:T(8,128)} %get-tuple-element.50, f32[3,33,96,256]{3,2,1,0:T(8,128)} %get-tuple-element.65, ...), kind=kLoop, calls=%fused_computation.7 | loop fusion | flops 25952256 | bytes 38597120 | tf_op jit(solution)/shard_map/sqrt | solution.py:44
  92.4 1.9 pad_maximum_fusion.2
  94.3 4.8 %all-to-all-start = ((f32[4,32,24,256]{3,2,1,0:T(8,128)}), f32[4,32,24,256]{3,2,1,0:T(8,128)S(1)}, u32[]{:S(2)}, u32[]{:S(2)}) async-start(f32[4,32,24,256]{3,2,1,0:T(8,128)} %pad_maximum_fusion.2), calls=%async_computation | async-start | bytes 6291456 | tf_op jit(solution)/shard_map/all_to_all | solution.py:75
  99.1 69.4 %all-to-all-done = f32[4,32,24,256]{3,2,1,0:T(8,128)S(1)} async-done(((f32[4,32,24,256]{3,2,1,0:T(8,128)}), f32[4,32,24,256]{3,2,1,0:T(8,128)S(1)}, u32[]{:S(2)}, u32[]{:S(2)}) %all-to-all-start) | async-done | bytes 3145760 | tf_op jit(solution)/shard_map/all_to_all | solution.py:75
  168.5 3.7 %copy.55 = f32[32,24,4,256]{3,2,1,0:T(4,128)} copy(f32[32,24,4,256]{3,1,0,2:T(8,128)S(1)} %bitcast.85) | data formatting | bytes 6291456 | tf_op jit(solution)/shard_map/reshape | solution.py:74
  172.2 5.2 %reshape_reshape.3 = f32[16,2,24,1024]{3,2,1,0:T(8,128)} reshape(f32[32,24,4,256]{3,2,1,0:T(4,128)} %copy.55) | data formatting | bytes 6291456 | tf_op jit(solution)/shard_map/reshape;reshape | solution.py:51
  177.4 3.5 %reduce_sum.90 = f32[16,24,1024]{2,1,0:T(8,128)} reduce(f32[16,2,24,1024]{3,2,1,0:T(8,128)} %reshape_reshape.3, f32[]{:T(128)} %constant.81.clone.1), dimensions={1}, to_apply=%region_0.1 | reduce | flops 393216 | bytes 4718596 | tf_op jit(solution)/shard_map/reduce_sum | solution.py:51
  180.9 3.5 %copy.67 = f32[16,24,1024]{2,0,1:T(8,128)} copy(f32[16,24,1024]{2,1,0:T(8,128)} %reduce_sum.90) | data formatting | bytes 3145728 | tf_op jit(solution)/shard_map/reshape | solution.py:52
  184.4 2.5 %reduce_sum.91 = f32[16,12,1024]{2,0,1:T(8,128)} reduce(f32[16,12,2,1024]{3,0,2,1:T(8,128)} %bitcast.87, f32[]{:T(128)} %constant.81.clone.1), dimensions={2}, to_apply=%region_1.2 | reduce | flops 196608 | bytes 2359300 | tf_op jit(solution)/shard_map/reduce_sum | solution.py:52
  186.8 3.0 %fusion.25 = f32[16,12,512]{2,0,1:T(8,128)} fusion(f32[16,12,1024]{2,0,1:T(8,128)} %reduce_sum.91, s32[1024]{0:T(1024)S(1)} %get-tuple-element.85, s32[1024]{0:T(1024)S(1)} %get-tuple-element.86, pred[1024]{0:T(1024)(128)(4,1)S(1)} %fusion.55), kind=kOutput, calls=%fused_computation.37 | convolution fusion | flops 1209106432 | bytes 1188864 | tf_op jit(solution)/shard_map/dot_general | solution.py:57
  190.0 2.1 copy.71
  192.1 32.9 %all-gather.2.cloned.1.call-done = f32[16,48,512]{2,0,1:T(8,128)} async-done(((f32[16,12,512]{2,0,1:T(8,128)}), f32[16,48,512]{2,0,1:T(8,128)}) %all-gather.2.cloned.1.call-update) | async-done | bytes 1572880 | tf_op jit(solution)/shard_map/all_gather | solution.py:78
  225.0 2.2 reshape.95
  227.3 3.0 %reduce_sum.92 = f32[8,48,512]{2,0,1:T(8,128)} reduce(f32[8,2,48,512]{3,1,0,2:T(2,128)S(1)} %reshape.95, f32[]{:T(128)} %constant.81.clone.1), dimensions={1}, to_apply=%region_2.3 | reduce | flops 196608 | bytes 2359300 | tf_op jit(solution)/shard_map/reduce_sum | solution.py:51
  230.2 1.2 reduce_sum.93
  231.5 1.4 bitcast_reduce_fusion
  235.5 2.1 copy.63
  (49 shorter events, 4.9 us)
Async XLA Ops:
  8.3 45.4 %collective-permute-start = (f32[3,1,96,256]{3,2,1,0:T(8,128)S(1)}, f32[3,1,96,256]{3,2,1,0:T(8,128)S(1)}, u32[]{:S(2)}, u32[]{:S(2)}) collective-permute-start(f32[3,1,96,256]{3,2,1,0:T(8,128)S(1)} %get-tuple-element.52), channel_id=1, source_target_pairs={{0,8},{8,16},{16,24},{24,0},{1,9},{9,17},{17,25},{25,1},{2,10},{10... | collective-permute-start | bytes 884744 | tf_op jit(solution)/shard_map/ppermute | solution.py:14
  8.8 57.3 %collective-permute-start.1 = (f32[3,1,96,256]{3,2,1,0:T(8,128)S(1)}, f32[3,1,96,256]{3,2,1,0:T(8,128)S(1)}, u32[]{:S(2)}, u32[]{:S(2)}) collective-permute-start(f32[3,1,96,256]{3,2,1,0:T(8,128)S(1)} %get-tuple-element.51), channel_id=1, source_target_pairs={{8,0},{16,8},{24,16},{0,24},{9,1},{17,9},{25,17},{1,25},{10,2},{18... | collective-permute-start | bytes 884744 | tf_op jit(solution)/shard_map/ppermute | solution.py:15
  22.6 31.0 %collective-permute-start.4 = (f32[3,32,96,1]{2,1,3,0:T(8,128)S(1)}, f32[3,32,96,1]{2,1,3,0:T(8,128)S(1)}, u32[]{:S(2)}, u32[]{:S(2)}) collective-permute-start(f32[3,32,96,1]{2,1,3,0:T(8,128)S(1)} %copy.69), channel_id=1, source_target_pairs={{1,0},{2,1},{3,2},{0,3},{5,4},{6,5},{7,6},{4,7},{9,8},{10,9},{11,1... | collective-permute-start | bytes 110600 | tf_op jit(solution)/shard_map/ppermute | solution.py:15
  30.1 40.5 %collective-permute-start.5 = (f32[3,32,96,1]{2,1,3,0:T(8,128)S(1)}, f32[3,32,96,1]{2,1,3,0:T(8,128)S(1)}, u32[]{:S(2)}, u32[]{:S(2)}) collective-permute-start(f32[3,32,96,1]{2,1,3,0:T(8,128)S(1)} %copy.70), channel_id=1, source_target_pairs={{0,1},{1,2},{2,3},{3,0},{4,5},{5,6},{6,7},{7,4},{8,9},{9,10},{10,1... | collective-permute-start | bytes 110600 | tf_op jit(solution)/shard_map/ppermute | solution.py:14
  36.5 18.1 %slice-start = ((s8[9437184]{0:T(1024)(128)(4,1)}), s8[4194304]{0:T(1024)(128)(4,1)S(1)}, s32[]{:S(2)}) async-start(s8[9437184]{0:T(1024)(128)(4,1)} %bitcast.83), calls=%async_computation.2 | async-start | bytes 8388608
  36.5 18.1 %slice-start.1 = ((s8[9437184]{0:T(1024)(128)(4,1)}), s8[1048576]{0:T(1024)(128)(4,1)S(1)}, s32[]{:S(2)}) async-start(s8[9437184]{0:T(1024)(128)(4,1)} %bitcast.83), calls=%async_computation.3 | async-start | bytes 2097152
  47.6 7.0 %slice-start.2 = ((s8[9437184]{0:T(1024)(128)(4,1)}), s8[4194304]{0:T(1024)(128)(4,1)S(1)}, s32[]{:S(2)}) async-start(s8[9437184]{0:T(1024)(128)(4,1)} %bitcast.83), calls=%async_computation.4 | async-start | bytes 8388608
  54.6 20.8 %copy-start = (f32[32,96,255]{2,1,0:T(8,128)S(1)}, f32[32,96,255]{2,1,0:T(8,128)}, u32[]{:S(2)}) copy-start(f32[32,96,255]{2,1,0:T(8,128)} %get-tuple-element.59) | copy-start | bytes 9400324
  54.6 20.8 %copy-start.1 = (f32[32,96,255]{2,1,0:T(8,128)S(1)}, f32[32,96,255]{2,1,0:T(8,128)}, u32[]{:S(2)}) copy-start(f32[32,96,255]{2,1,0:T(8,128)} %get-tuple-element.60) | copy-start | bytes 9400324
  68.6 5.7 %collective-permute-start.2 = (f32[3,34,1,256]{3,2,1,0:T(1,128)S(1)}, f32[3,34,1,256]{3,2,1,0:T(1,128)S(1)}, u32[]{:S(2)}, u32[]{:S(2)}) collective-permute-start(f32[3,34,1,256]{3,2,1,0:T(1,128)S(1)} %get-tuple-element.42), channel_id=1, source_target_pairs={{4,0},{0,4},{5,1},{1,5},{6,2},{2,6},{7,3},{3,7},{12,8},{8,12},{13,... | collective-permute-start | bytes 313352 | tf_op jit(solution)/shard_map/ppermute | solution.py:15
  70.1 5.3 %collective-permute-start.3 = (f32[3,34,1,256]{3,2,1,0:T(1,128)S(1)}, f32[3,34,1,256]{3,2,1,0:T(1,128)S(1)}, u32[]{:S(2)}, u32[]{:S(2)}) collective-permute-start(f32[3,34,1,256]{3,2,1,0:T(1,128)S(1)} %get-tuple-element.43), channel_id=1, source_target_pairs={{0,4},{4,0},{1,5},{5,1},{2,6},{6,2},{3,7},{7,3},{8,12},{12,8},{9,1... | collective-permute-start | bytes 313352 | tf_op jit(solution)/shard_map/ppermute | solution.py:14
  94.3 74.2 %all-to-all-start = ((f32[4,32,24,256]{3,2,1,0:T(8,128)}), f32[4,32,24,256]{3,2,1,0:T(8,128)S(1)}, u32[]{:S(2)}, u32[]{:S(2)}) async-start(f32[4,32,24,256]{3,2,1,0:T(8,128)} %pad_maximum_fusion.2), calls=%async_computation | async-start | bytes 6291456 | tf_op jit(solution)/shard_map/all_to_all | solution.py:75
  99.1 125.9 %all-gather.2.cloned.1.call-start = ((), (), s32[]{:S(2)}) async-start(), calls=%async_computation.1 | async-start | bytes 1966080 | tf_op jit(solution)/shard_map/all_gather | solution.py:78
  227.2 8.3 %copy-start.2 = (f32[16,48,512]{2,0,1:T(8,128)S(1)}, f32[16,48,512]{2,0,1:T(8,128)}, u32[]{:S(2)}) copy-start(f32[16,48,512]{2,0,1:T(8,128)} %all-gather.2.cloned.1.call-done) | copy-start | bytes 4718596
Sparse Core Ops, SparseCore 0:
  190.0 34.9 all-gather.1
